TPU v7x, 32 devices: a whole 2x2x4 slice. The times are simulated.
32 devices in a mesh: batch: 4 (over x, core), space: 8 (over z, y).
Axes of the slice: x: 2, y: 2, z: 4, core: 2. Of those that a mesh axis runs over, the one named last changes fastest.
Arguments:
- inputs: bfloat16 [4, 128, 64, 64, 128], P('batch', 'space'), may hold values from -6 to 6
- cotangent: bfloat16 [4, 128, 64, 64, 128], P('batch', 'space'), may hold values from -6 to 6
- mode_weights: bfloat16 [256, 16, 64, 128], P('space'), may hold values from -1.5 to 1.5
Outputs:
- input_grad: bfloat16 [4, 128, 64, 64, 128], P('batch', 'space')
- weight_grad: float32 [256, 16, 64, 128], P('space')
All inputs are finite; a program needn't handle non-finite values.
Results may differ from a plain program's by a relative error of at most 0.015.
Values may be sent and summed in bfloat16 or wider, within the bound.
No kernel may reach another device: no remote copies, remote signals or barrier semaphores. Data moves between devices by JAX's collectives and lax.ppermute only.
A program may use at most 192 MiB of HBM per device.

v0:
```python
import math
import jax
import jax.numpy as jnp
from jax import lax
from jax.sharding import PartitionSpec as P

C = 64
X = 64
Y = 128
Z = 128
MX = 16
MY = 16
MZ = 16
two_pi = 2.0 * math.pi
highest = lax.Precision.HIGHEST


def twiddles(wave_list, positions, length):
    product = wave_list[:, None] * positions[None, :] % length
    angles = two_pi / length * product.astype(jnp.float32)
    return (jnp.cos(angles), jnp.sin(angles))


def wave_pair(retained, length):
    return jnp.concatenate([jnp.arange(retained // 2), jnp.arange(length - retained // 2, length)])


def plane_spectrum(values, z_table, cos_x, sin_x, factor):
    lead_dims = values.shape[:-3]
    along_z = jnp.dot(values.reshape(-1, Z), z_table, preferred_element_type=jnp.float32)
    along_z = along_z.reshape(lead_dims + (C, X, 2 * MZ))
    first_term = jnp.einsum("kx,...cxm->...ckm", cos_x, along_z, precision=highest)
    second_term = jnp.einsum("kx,...cxm->...ckm", sin_x, along_z, precision=highest)
    real_part = (first_term[..., :MZ] + second_term[..., MZ:]) * factor
    imag_part = (first_term[..., MZ:] - second_term[..., :MZ]) * factor
    stacked = jnp.stack([real_part, imag_part], axis=-4)
    return stacked.reshape(lead_dims + (2, C, MX * MZ)).astype(jnp.bfloat16)


def modes_along_y(spectra, cos_y, sin_y):
    values_f = spectra.astype(jnp.float32)
    real_in = values_f[:, :, 0]
    imag_in = values_f[:, :, 1]
    real_out = jnp.einsum("ky,bycp->pbkc", cos_y, real_in, precision=highest) + jnp.einsum(
        "ky,bycp->pbkc", sin_y, imag_in, precision=highest
    )
    imag_out = jnp.einsum("ky,bycp->pbkc", cos_y, imag_in, precision=highest) - jnp.einsum(
        "ky,bycp->pbkc", sin_y, real_in, precision=highest
    )
    return jnp.stack([real_out, imag_out], axis=3)


def planes_along_y(mode_data, cos_y, sin_y):
    values_f = mode_data.astype(jnp.float32)
    real_in = values_f[:, :, :, 0]
    imag_in = values_f[:, :, :, 1]
    real_out = jnp.einsum("ky,pbkc->bycp", cos_y, real_in, precision=highest) - jnp.einsum(
        "ky,pbkc->bycp", sin_y, imag_in, precision=highest
    )
    imag_out = jnp.einsum("ky,pbkc->bycp", sin_y, real_in, precision=highest) + jnp.einsum(
        "ky,pbkc->bycp", cos_y, imag_in, precision=highest
    )
    return jnp.stack([real_out, imag_out], axis=2)


def plane_inverse(spectra, cos_x, sin_x, z_back):
    lead_dims = spectra.shape[:-3]
    values_f = spectra.astype(jnp.float32).reshape(lead_dims + (2, C, MX, MZ))
    real_in = values_f[..., 0, :, :, :]
    imag_in = values_f[..., 1, :, :, :]
    real_out = jnp.einsum("kx,...ckm->...cxm", cos_x, real_in, precision=highest) - jnp.einsum(
        "kx,...ckm->...cxm", sin_x, imag_in, precision=highest
    )
    imag_out = jnp.einsum("kx,...ckm->...cxm", sin_x, real_in, precision=highest) + jnp.einsum(
        "kx,...ckm->...cxm", cos_x, imag_in, precision=highest
    )
    joined = jnp.concatenate([real_out, imag_out], axis=-1)
    result = jnp.dot(
        joined.reshape(-1, 2 * MZ), z_back, precision=highest, preferred_element_type=jnp.float32
    )
    return result.reshape(lead_dims + (C, X, Z)).astype(jnp.bfloat16)


def split_cot(cot_modes):
    real_part = cot_modes[:, :, :, 0]
    imag_part = cot_modes[:, :, :, 1]
    return (
        jnp.concatenate([real_part, imag_part], axis=-1),
        jnp.concatenate([imag_part, -real_part], axis=-1),
    )


def weight_terms(input_modes, cot_modes):
    cot_one, cot_two = split_cot(cot_modes)
    first_term = jnp.einsum(
        "pbki,pbkj->pkij", input_modes[:, :, :, 0], cot_one, preferred_element_type=jnp.float32
    )
    second_term = jnp.einsum(
        "pbki,pbkj->pkij", input_modes[:, :, :, 1], cot_two, preferred_element_type=jnp.float32
    )
    return first_term + second_term


def local(inputs, cotangent, mode_weights):
    inv_scale = 1.0 / math.sqrt(X * Y * Z)
    cos_z, sin_z = twiddles(jnp.arange(MZ), jnp.arange(Z), Z)
    z_table = jnp.concatenate([cos_z.T, -sin_z.T], axis=1).astype(jnp.bfloat16)
    z_back = jnp.concatenate([cos_z, -sin_z], axis=0) * inv_scale
    cos_x, sin_x = twiddles(wave_pair(MX, X), jnp.arange(X), X)
    plain_z = jnp.full((MZ,), inv_scale, jnp.float32)
    weight_z = jnp.where(jnp.arange(MZ) == 0, 1.0, 2.0).astype(jnp.float32) * inv_scale
    input_spec = plane_spectrum(inputs, z_table, cos_x, sin_x, plain_z)
    cot_spec = plane_spectrum(cotangent, z_table, cos_x, sin_x, weight_z)
    y_waves = wave_pair(MY, Y)
    positions = jnp.arange(Y)
    cos_y, sin_y = twiddles(y_waves, positions, Y)
    moved_input, moved_cot = (
        lax.all_to_all(input_spec, "space", split_axis=4, concat_axis=1, tiled=True),
        lax.all_to_all(cot_spec, "space", split_axis=4, concat_axis=1, tiled=True),
    )
    input_modes = modes_along_y(moved_input, cos_y, sin_y)
    cot_modes = modes_along_y(moved_cot, cos_y, sin_y)
    input_modes = input_modes.astype(jnp.bfloat16)
    cot_modes = cot_modes.astype(jnp.bfloat16)
    weight_grad = lax.psum(
        weight_terms(input_modes, cot_modes).astype(jnp.bfloat16), "batch"
    ).astype(jnp.float32)
    cot_one, cot_two = split_cot(cot_modes)
    grad_real = jnp.einsum(
        "pbkj,pkij->pbki", cot_one, mode_weights, preferred_element_type=jnp.float32
    )
    grad_imag = jnp.einsum(
        "pbkj,pkij->pbki", cot_two, mode_weights, preferred_element_type=jnp.float32
    )
    mode_grad = jnp.stack([grad_real, grad_imag], axis=3).astype(jnp.bfloat16)
    plane_modes = planes_along_y(mode_grad, cos_y, sin_y).astype(jnp.bfloat16)
    back_spec = lax.all_to_all(plane_modes, "space", split_axis=1, concat_axis=4, tiled=True)
    input_grad = plane_inverse(back_spec, cos_x, sin_x, z_back)
    return (input_grad, weight_grad)


def solution(mesh):
    placed = (
        P("batch", "space", None, None, None),
        P("batch", "space", None, None, None),
        P("space", None, None, None),
    )
    return jax.shard_map(
        local,
        mesh=mesh,
        in_specs=placed,
        out_specs=(P("batch", "space", None, None, None), P("space", None, None, None)),
        check_vma=False,
    )
```

profile of v0, /device:TPU:0, one launch (start us, length us, event | category | flops | bytes accessed | tf_op | source)
XLA Modules:
  0.0 509.5 jit_solution(14194246704716014748)
XLA Ops:
  7.2 15.0 %convolution_bitcast_fusion.1 = f32[65536,32]{0,1:T(8,128)} fusion(bf16[65536,128]{1,0:T(8,128)(2,1)} %bitcast.208, bf16[128,16]{0,1:T(8,128)(2,1)S(1)} %get-tuple-element.24, bf16[128,16]{0,1:T(8,128)(2,1)S(1)} %get-tuple-element.25), kind=kOutput, calls=%fused_computation.1 | convolution fusion | flops 536887296 | bytes 25174016 | tf_op jit(solution)/shard_map/dot_general | solution.py:30
  22.3 12.2 %reshape.397 = f32[16,64,64,32]{2,1,0,3:T(8,128)} reshape(f32[65536,32]{0,1:T(8,128)} %convolution_bitcast_fusion.1) | data formatting | bytes 16777216 | tf_op jit(solution)/shard_map/reshape
  34.5 41.9 %fusion.15 = f32[1,16,64,16,32]{2,3,4,1,0:T(8,128)S(1)} fusion(f32[16,64,64,32]{2,1,0,3:T(8,128)} %reshape.397, s32[16]{0:T(128)S(1)} %get-tuple-element.21), kind=kOutput, calls=%fused_computation.18 | convolution fusion | flops 402667520 | bytes 10485824 | tf_op jit(solution)/shard_map/kx,...cxm->...ckm/dot_general | solution.py:33
  76.5 39.9 %fusion.12 = f32[1,16,64,16,32]{2,3,4,1,0:T(8,128)S(1)} fusion(f32[16,64,64,32]{2,1,0,3:T(8,128)S(1)} %copy-done, s32[16]{0:T(128)S(1)} %get-tuple-element.21), kind=kOutput, calls=%fused_computation.17 | convolution fusion | flops 402667520 | bytes 10485824 | tf_op jit(solution)/shard_map/kx,...cxm->...ckm/dot_general | solution.py:32
  122.4 7.3 %all-to-all-start = ((bf16[8,2,32768]{2,1,0:T(2,128)(2,1)}), bf16[8,2,32768]{2,1,0:T(2,128)(2,1)S(1)}, u32[]{:S(2)}, u32[]{:S(2)}) async-start(bf16[8,2,32768]{2,1,0:T(2,128)(2,1)} %reshape.424), calls=%async_computation | async-start | bytes 2097152 | tf_op jit(solution)/shard_map/all_to_all | solution.py:119
  129.7 15.0 %convolution_bitcast_fusion = f32[65536,32]{0,1:T(8,128)} fusion(bf16[65536,128]{1,0:T(8,128)(2,1)} %bitcast.209, bf16[128,16]{0,1:T(8,128)(2,1)S(1)} %get-tuple-element.24, bf16[128,16]{0,1:T(8,128)(2,1)S(1)} %get-tuple-element.25), kind=kOutput, calls=%fused_computation | convolution fusion | flops 536887296 | bytes 25174016 | tf_op jit(solution)/shard_map/dot_general | solution.py:30
  144.7 12.2 %reshape.406 = f32[16,64,64,32]{2,1,0,3:T(8,128)} reshape(f32[65536,32]{0,1:T(8,128)} %convolution_bitcast_fusion) | data formatting | bytes 16777216 | tf_op jit(solution)/shard_map/reshape.48
  157.0 41.9 %fusion.21 = f32[1,16,64,16,32]{2,3,4,1,0:T(8,128)S(1)} fusion(f32[16,64,64,32]{2,1,0,3:T(8,128)} %reshape.406, s32[16]{0:T(128)S(1)} %get-tuple-element.21), kind=kOutput, calls=%fused_computation.20 | convolution fusion | flops 402667520 | bytes 10485824 | tf_op jit(solution)/shard_map/kx,...cxm->...ckm/dot_general | solution.py:33
  198.9 39.6 %fusion.18 = f32[1,16,64,16,32]{2,3,4,1,0:T(8,128)S(1)} fusion(f32[16,64,64,32]{2,1,0,3:T(8,128)S(1)} %copy-done.1, s32[16]{0:T(128)S(1)} %get-tuple-element.21), kind=kOutput, calls=%fused_computation.19 | convolution fusion | flops 402667520 | bytes 10485824 | tf_op jit(solution)/shard_map/kx,...cxm->...ckm/dot_general | solution.py:32
  245.3 6.0 %all-to-all-start.2 = ((bf16[8,2,32768]{2,1,0:T(2,128)(2,1)}), bf16[8,2,32768]{2,1,0:T(2,128)(2,1)S(1)}, u32[]{:S(2)}, u32[]{:S(2)}) async-start(bf16[8,2,32768]{2,1,0:T(2,128)(2,1)} %reshape.428), calls=%async_computation.2 | async-start | bytes 2097152 | tf_op jit(solution)/shard_map/all_to_all | solution.py:118
  258.0 3.6 copy.109
  261.6 3.6 copy.108
  274.5 7.8 %fusion.64 = f32[32,16,1,64]{3,2,1,0:T(1,128)S(1)} fusion(bf16[32,16,64,128]{3,2,1,0:T(8,128)(2,1)} %param.5, bf16[32,16,128,1]{2,1,0,3:T(8,128)(2,1)S(1)} %get-tuple-element.15), kind=kOutput, calls=%fused_computation.76 | convolution fusion | flops 8388608 | bytes 8650752 | tf_op jit(solution)/shard_map/pbkj,pkij->pbki/dot_general | solution.py:129
  283.1 8.2 %fusion.62 = f32[32,16,1,64]{3,2,1,0:T(1,128)S(1)} fusion(bf16[32,16,64,128]{3,2,1,0:T(8,128)(2,1)} %param.5, bf16[32,16,128,1]{2,1,0,3:T(8,128)(2,1)S(1)} %get-tuple-element.18), kind=kOutput, calls=%fused_computation.74 | convolution fusion | flops 8388608 | bytes 8650752 | tf_op jit(solution)/shard_map/pbkj,pkij->pbki/dot_general | solution.py:132
  294.8 3.9 copy.81
  301.4 6.0 %all-to-all-start.1 = ((bf16[8,2,32768]{2,1,0:T(2,128)(2,1)}), bf16[8,2,32768]{2,1,0:T(2,128)(2,1)}, u32[]{:S(2)}, u32[]{:S(2)}) async-start(bf16[8,2,32768]{2,1,0:T(2,128)(2,1)} %reshape.426), calls=%async_computation.1 | async-start | bytes 2097152 | tf_op jit(solution)/shard_map/all_to_all | solution.py:137
  323.4 12.6 %add_convert_fusion = bf16[32,16,64,128]{3,2,1,0:T(8,128)(2,1)} fusion(f32[32,16,128]{2,1,0:T(8,128)} %get-tuple-element.19, f32[32,16,64]{2,1,0:T(8,128)S(1)} %copy.96, f32[32,16,128]{2,1,0:T(8,128)S(1)} %get-tuple-element.14, f32[32,16,64]{2,1,0:T(8,128)S(1)} %copy.95), kind=kLoop, calls=%fused_computation.5 | loop fusion | flops 16777216 | bytes 9175040 | tf_op jit(solution)/shard_map/convert_element_type | solution.py:126
  340.3 4.4 fusion.51
  344.7 4.4 fusion.52
  349.2 5.2 %add_bitcast_fusion = f32[1,16,64,64,16]{3,2,4,1,0:T(8,128)S(1)} fusion(f32[16,64,16,64]{3,1,2,0:T(8,128)S(1)} %fusion.51, bf16[1,16,1,64,16,16]{3,5,4,2,1,0:T(8,128)(2,1)S(1)} %get-tuple-element.8, s32[16]{0:T(128)S(1)} %get-tuple-element.21), kind=kOutput, calls=%fused_computation.15 | convolution fusion | flops 202389504 | bytes 8912960 | tf_op jit(solution)/shard_map/kx,...ckm->...cxm/dot_general | solution.py:74
  354.4 4.9 subtract_bitcast_fusion
  362.6 58.2 %convert_bitcast_fusion = bf16[1,16,64,64,128]{4,3,2,1,0:T(8,128)(2,1)} fusion(f32[16,64,64,32]{2,1,3,0:T(8,128)S(1)} %maximum_bitcast_fusion, f32[16,128]{1,0:T(8,128)S(1)} %get-tuple-element.28, f32[16,128]{1,0:T(8,128)S(1)} %get-tuple-element.29), kind=kOutput, calls=%fused_computation.6 | convolution fusion | flops 3229622272 | bytes 25182208 | tf_op jit(solution)/shard_map/dot_general | solution.py:78
  420.8 69.6 %all-reduce.2.cloned.1.call-done = bf16[32,16,64,128]{3,2,1,0:T(8,128)(2,1)} async-done(((bf16[32,16,64,128]{3,2,1,0:T(8,128)(2,1)}), bf16[32,16,64,128]{3,2,1,0:T(8,128)(2,1)}) %all-reduce.2.cloned.1.call-update) | async-done | bytes 8388624 | tf_op jit(solution)/shard_map/psum | solution.py:125
  490.4 11.7 %convert_element_type.95 = f32[32,16,64,128]{3,2,1,0:T(8,128)} convert(bf16[32,16,64,128]{3,2,1,0:T(8,128)(2,1)} %all-reduce.2.cloned.1.call-done) | non-fusion elementwise | flops 4194304 | bytes 25165824 | tf_op jit(solution)/shard_map/convert_element_type | solution.py:127
  (61 shorter events, 59.3 us)
Async XLA Ops:
  34.5 42.0 %copy-start = (f32[16,64,64,32]{2,1,0,3:T(8,128)S(1)}, f32[16,64,64,32]{2,1,0,3:T(8,128)}, u32[]{:S(2)}) copy-start(f32[16,64,64,32]{2,1,0,3:T(8,128)} %reshape.397) | copy-start | bytes 25165828
  122.4 121.9 %all-to-all-start = ((bf16[8,2,32768]{2,1,0:T(2,128)(2,1)}), bf16[8,2,32768]{2,1,0:T(2,128)(2,1)S(1)}, u32[]{:S(2)}, u32[]{:S(2)}) async-start(bf16[8,2,32768]{2,1,0:T(2,128)(2,1)} %reshape.424), calls=%async_computation | async-start | bytes 2097152 | tf_op jit(solution)/shard_map/all_to_all | solution.py:119
  157.0 41.9 %copy-start.1 = (f32[16,64,64,32]{2,1,0,3:T(8,128)S(1)}, f32[16,64,64,32]{2,1,0,3:T(8,128)}, u32[]{:S(2)}) copy-start(f32[16,64,64,32]{2,1,0,3:T(8,128)} %reshape.406) | copy-start | bytes 25165828
  244.4 1.0 copy-start.2
  245.3 56.1 %all-to-all-start.2 = ((bf16[8,2,32768]{2,1,0:T(2,128)(2,1)}), bf16[8,2,32768]{2,1,0:T(2,128)(2,1)S(1)}, u32[]{:S(2)}, u32[]{:S(2)}) async-start(bf16[8,2,32768]{2,1,0:T(2,128)(2,1)} %reshape.428), calls=%async_computation.2 | async-start | bytes 2097152 | tf_op jit(solution)/shard_map/all_to_all | solution.py:118
  301.4 34.7 %all-to-all-start.1 = ((bf16[8,2,32768]{2,1,0:T(2,128)(2,1)}), bf16[8,2,32768]{2,1,0:T(2,128)(2,1)}, u32[]{:S(2)}, u32[]{:S(2)}) async-start(bf16[8,2,32768]{2,1,0:T(2,128)(2,1)} %reshape.426), calls=%async_computation.1 | async-start | bytes 2097152 | tf_op jit(solution)/shard_map/all_to_all | solution.py:137
  307.4 183.0 %all-reduce.2.cloned.1.call-start = ((), (), s32[]{:S(2)}) async-start(), calls=%async_computation.3 | async-start | bytes 16777216 | tf_op jit(solution)/shard_map/psum | solution.py:125
Sparse Core Ops, SparseCore 0:
  336.2 154.2 all-reduce.1
where the time goes:
time: 517 us; the launch traced here: 509 us
  matrix products  307 us (59%)
  waiting for transfers between devices  69.6 us (13%)
  local copies, waits for them, and re-layouts  66.4 us (13%)
  other arithmetic  32.5 us (6%)
  starting transfers between devices  19.3 us (4%)
  between operations  14.8 us (3%)
    dot_general x2, matrix products, plane_spectrum(): jnp.einsum('kx,...cxm->...ckm', sin_x, along_z, precision=highest)  83.9 us
    dot_general x2, matrix products, plane_spectrum(): jnp.einsum('kx,...cxm->...ckm', cos_x, along_z, precision=highest)  79.5 us
    psum x1, waiting for transfers between devices, local(): lax.psum(weight_terms(input_modes, cot_modes).astype(jnp.bfloat16), 'batch')  69.6 us
    dot_general x1, matrix products, plane_inverse(): jnp.dot(joined.reshape(-1, 2 * MZ), z_back, precision=highest, preferred_...  58.2 us
    dot_general x2, matrix products, plane_spectrum(): jnp.dot(values.reshape(-1, Z), z_table, preferred_element_type=jnp.float32)  30 us
    unnamed x16, local copies, waits for them, and re-layouts  27.2 us
    another operation x8, local copies, waits for them, and re-layouts  15.9 us
    convert_element_type x1, other arithmetic, local(): weight_terms(input_modes, cot_modes).astype(jnp.bfloat16)  12.6 us
  transfers between devices with their start and end apart: 4, of which 1 were waited for; matrix products, arithmetic and copies ran while one was open for 55% of the time, Pallas kernels for 0%

commit v1 on v0

--- a/solution.py
+++ b/solution.py
@@ -13,6 +13,12 @@
 MZ = 16
 two_pi = 2.0 * math.pi
 highest = lax.Precision.HIGHEST
+
+
+def gather_and_add(block, name):
+    parts = lax.all_gather(block, name, axis=0, tiled=False)
+    total = parts.sum(axis=0)
+    return total
 
 
 def twiddles(wave_list, positions, length):
@@ -122,7 +128,7 @@
     cot_modes = modes_along_y(moved_cot, cos_y, sin_y)
     input_modes = input_modes.astype(jnp.bfloat16)
     cot_modes = cot_modes.astype(jnp.bfloat16)
-    weight_grad = lax.psum(
+    weight_grad = gather_and_add(
         weight_terms(input_modes, cot_modes).astype(jnp.bfloat16), "batch"
     ).astype(jnp.float32)
     cot_one, cot_two = split_cot(cot_modes)

time: 517 us -> 554 us (1.072)
  waiting for transfers between devices: 69.6 us -> 94.1 us
  other arithmetic: 32.5 us -> 46.5 us
    psum x1 -> x0, waiting for transfers between devices: 69.6 us -> none  [local(): lax.psum(weight_terms(input_modes, cot_modes).astype(jnp.bfloat16), 'batch')]
    all_gather x0 -> x1, waiting for transfers between devices: none -> 60.8 us  [gather_and_add(): parts = lax.all_gather(block, name, axis=0, tiled=False)]
    all_to_all x1, waiting for transfers between devices: 0.01 us -> 25.9 us  [local(): lax.all_to_all(plane_modes, 'space', split_axis=1, concat_axis=4, tiled=T...]
    reduce_sum x0 -> x1, other arithmetic: none -> 16.4 us  [gather_and_add(): total = parts.sum(axis=0)]
    all_to_all x1, waiting for transfers between devices: 0.01 us -> 7.47 us  [local(): lax.all_to_all(input_spec, 'space', split_axis=4, concat_axis=1, tiled=True)]
    unnamed x16 -> x14, local copies, waits for them, and re-layouts: 27.2 us -> 24.8 us
  transfers between devices with their start and end apart: 4 -> 4, of which waited for: 1 -> 3; matrix products, arithmetic and copies ran while one was open for 55% -> 44% of each run, Pallas kernels for 0% -> 0%
where the time goes in v1:
time: 554 us; the launch traced here: 546 us
  matrix products  309 us (56%)
  waiting for transfers between devices  94.1 us (17%)
  local copies, waits for them, and re-layouts  64.7 us (12%)
  other arithmetic  46.5 us (8%)
  starting transfers between devices  17.2 us (3%)
  between operations  14.6 us (3%)
    dot_general x2, matrix products, plane_spectrum(): jnp.einsum('kx,...cxm->...ckm', sin_x, along_z, precision=highest)  83.9 us
    dot_general x2, matrix products, plane_spectrum(): jnp.einsum('kx,...cxm->...ckm', cos_x, along_z, precision=highest)  79.7 us
    all_gather x1, waiting for transfers between devices, gather_and_add(): parts = lax.all_gather(block, name, axis=0, tiled=False)  60.8 us
    dot_general x1, matrix products, plane_inverse(): jnp.dot(joined.reshape(-1, 2 * MZ), z_back, precision=highest, preferred_...  58.2 us
    dot_general x2, matrix products, plane_spectrum(): jnp.dot(values.reshape(-1, Z), z_table, preferred_element_type=jnp.float32)  30 us
    all_to_all x1, waiting for transfers between devices, local(): lax.all_to_all(plane_modes, 'space', split_axis=1, concat_axis=4, tiled=T...  25.9 us
    unnamed x14, local copies, waits for them, and re-layouts  24.8 us
    another operation x8, local copies, waits for them, and re-layouts  16.5 us
  transfers between devices with their start and end apart: 4, of which 3 were waited for; matrix products, arithmetic and copies ran while one was open for 44% of the time, Pallas kernels for 0%

profile of v1, /device:TPU:0, one launch (start us, length us, event | category | flops | bytes accessed | tf_op | source)
XLA Modules:
  0.0 546.5 jit_solution(2213170119710773648)
XLA Ops:
  7.3 15.0 %convolution_bitcast_fusion.1 = f32[65536,32]{0,1:T(8,128)} fusion(bf16[65536,128]{1,0:T(8,128)(2,1)} %bitcast.209, bf16[128,16]{0,1:T(8,128)(2,1)S(1)} %get-tuple-element.24, bf16[128,16]{0,1:T(8,128)(2,1)S(1)} %get-tuple-element.25), kind=kOutput, calls=%fused_computation.1 | convolution fusion | flops 536887296 | bytes 25174016 | tf_op jit(solution)/shard_map/dot_general | solution.py:36
  22.3 12.2 %reshape.397 = f32[16,64,64,32]{2,1,0,3:T(8,128)} reshape(f32[65536,32]{0,1:T(8,128)} %convolution_bitcast_fusion.1) | data formatting | bytes 16777216 | tf_op jit(solution)/shard_map/reshape
  34.6 41.9 %fusion.15 = f32[1,16,64,16,32]{2,3,4,1,0:T(8,128)S(1)} fusion(f32[16,64,64,32]{2,1,0,3:T(8,128)} %reshape.397, s32[16]{0:T(128)S(1)} %get-tuple-element.21), kind=kOutput, calls=%fused_computation.18 | convolution fusion | flops 402667520 | bytes 10485824 | tf_op jit(solution)/shard_map/kx,...cxm->...ckm/dot_general | solution.py:39
  76.5 39.9 %fusion.12 = f32[1,16,64,16,32]{2,3,4,1,0:T(8,128)S(1)} fusion(f32[16,64,64,32]{2,1,0,3:T(8,128)S(1)} %copy-done, s32[16]{0:T(128)S(1)} %get-tuple-element.21), kind=kOutput, calls=%fused_computation.17 | convolution fusion | flops 402667520 | bytes 10485824 | tf_op jit(solution)/shard_map/kx,...cxm->...ckm/dot_general | solution.py:38
  122.4 7.3 %all-to-all-start = ((bf16[8,2,32768]{2,1,0:T(2,128)(2,1)}), bf16[8,2,32768]{2,1,0:T(2,128)(2,1)S(1)}, u32[]{:S(2)}, u32[]{:S(2)}) async-start(bf16[8,2,32768]{2,1,0:T(2,128)(2,1)} %reshape.425), calls=%async_computation | async-start | bytes 2097152 | tf_op jit(solution)/shard_map/all_to_all | solution.py:125
  129.7 15.0 %convolution_bitcast_fusion = f32[65536,32]{0,1:T(8,128)} fusion(bf16[65536,128]{1,0:T(8,128)(2,1)} %bitcast.210, bf16[128,16]{0,1:T(8,128)(2,1)S(1)} %get-tuple-element.24, bf16[128,16]{0,1:T(8,128)(2,1)S(1)} %get-tuple-element.25), kind=kOutput, calls=%fused_computation | convolution fusion | flops 536887296 | bytes 25174016 | tf_op jit(solution)/shard_map/dot_general | solution.py:36
  144.7 12.2 %reshape.406 = f32[16,64,64,32]{2,1,0,3:T(8,128)} reshape(f32[65536,32]{0,1:T(8,128)} %convolution_bitcast_fusion) | data formatting | bytes 16777216 | tf_op jit(solution)/shard_map/reshape.48
  156.9 41.9 %fusion.21 = f32[1,16,64,16,32]{2,3,4,1,0:T(8,128)S(1)} fusion(f32[16,64,64,32]{2,1,0,3:T(8,128)} %reshape.406, s32[16]{0:T(128)S(1)} %get-tuple-element.21), kind=kOutput, calls=%fused_computation.20 | convolution fusion | flops 402667520 | bytes 10485824 | tf_op jit(solution)/shard_map/kx,...cxm->...ckm/dot_general | solution.py:39
  198.9 39.8 %fusion.18 = f32[1,16,64,16,32]{2,3,4,1,0:T(8,128)S(1)} fusion(f32[16,64,64,32]{2,1,0,3:T(8,128)S(1)} %copy-done.1, s32[16]{0:T(128)S(1)} %get-tuple-element.21), kind=kOutput, calls=%fused_computation.19 | convolution fusion | flops 402667520 | bytes 10485824 | tf_op jit(solution)/shard_map/kx,...cxm->...ckm/dot_general | solution.py:38
  244.5 6.0 %all-to-all-start.2 = ((bf16[8,2,32768]{2,1,0:T(2,128)(2,1)}), bf16[8,2,32768]{2,1,0:T(2,128)(2,1)}, u32[]{:S(2)}, u32[]{:S(2)}) async-start(bf16[8,2,32768]{2,1,0:T(2,128)(2,1)} %reshape.429), calls=%async_computation.2 | async-start | bytes 2097152 | tf_op jit(solution)/shard_map/all_to_all | solution.py:124
  268.6 7.5 %all-to-all-done.2 = bf16[8,2,32768]{2,1,0:T(2,128)(2,1)} async-done(((bf16[8,2,32768]{2,1,0:T(2,128)(2,1)}), bf16[8,2,32768]{2,1,0:T(2,128)(2,1)}, u32[]{:S(2)}, u32[]{:S(2)}) %all-to-all-start.2) | async-done | bytes 1048608 | tf_op jit(solution)/shard_map/all_to_all | solution.py:124
  298.8 12.0 %add_convert_fusion = bf16[32,16,64,128]{3,2,1,0:T(8,128)(2,1)} fusion(f32[32,16,128]{2,1,0:T(8,128)S(1)} %get-tuple-element.19, f32[32,16,64]{2,1,0:T(8,128)S(1)} %copy.96, f32[32,16,128]{2,1,0:T(8,128)S(1)} %get-tuple-element.14, f32[32,16,64]{2,1,0:T(8,128)S(1)} %copy.95), kind=kLoop, calls=%fused_computation.5 | loop fusion | flops 16777216 | bytes 9175040 | tf_op jit(solution)/shard_map/convert_element_type | solution.py:132
  310.8 7.8 %fusion.64 = f32[32,16,1,64]{3,2,1,0:T(1,128)S(1)} fusion(bf16[32,16,64,128]{3,2,1,0:T(8,128)(2,1)} %param.5, bf16[32,16,128,1]{2,1,0,3:T(8,128)(2,1)S(1)} %get-tuple-element.15), kind=kOutput, calls=%fused_computation.76 | convolution fusion | flops 8388608 | bytes 8650752 | tf_op jit(solution)/shard_map/pbkj,pkij->pbki/dot_general | solution.py:135
  319.4 9.9 %fusion.62 = f32[32,16,1,64]{3,2,1,0:T(1,128)S(1)} fusion(bf16[32,16,64,128]{3,2,1,0:T(8,128)(2,1)} %param.5, bf16[32,16,128,1]{2,1,0,3:T(8,128)(2,1)S(1)} %get-tuple-element.18), kind=kOutput, calls=%fused_computation.74 | convolution fusion | flops 8388608 | bytes 8650752 | tf_op jit(solution)/shard_map/pbkj,pkij->pbki/dot_general | solution.py:138
  337.6 3.8 all-to-all-start.1
  341.4 25.9 %all-to-all-done.1 = bf16[8,2,32768]{2,1,0:T(2,128)(2,1)S(1)} async-done(((bf16[8,2,32768]{2,1,0:T(2,128)(2,1)}), bf16[8,2,32768]{2,1,0:T(2,128)(2,1)S(1)}, u32[]{:S(2)}, u32[]{:S(2)}) %all-to-all-start.1) | async-done | bytes 1048608 | tf_op jit(solution)/shard_map/all_to_all | solution.py:143
  370.0 4.4 fusion.51
  374.5 4.4 fusion.52
  378.9 5.1 add_bitcast_fusion
  384.1 4.9 subtract_bitcast_fusion
  392.4 58.2 %convert_bitcast_fusion = bf16[1,16,64,64,128]{4,3,2,1,0:T(8,128)(2,1)} fusion(f32[16,64,64,32]{2,1,3,0:T(8,128)S(1)} %maximum_bitcast_fusion, f32[16,128]{1,0:T(8,128)S(1)} %get-tuple-element.28, f32[16,128]{1,0:T(8,128)S(1)} %get-tuple-element.29), kind=kOutput, calls=%fused_computation.6 | convolution fusion | flops 3229622272 | bytes 25182208 | tf_op jit(solution)/shard_map/dot_general | solution.py:84
  450.5 60.8 %all-gather.3.cloned.1.call-done = bf16[128,16,64,128]{3,2,1,0:T(8,128)(2,1)} async-done(((bf16[32,16,64,128]{3,2,1,0:T(8,128)(2,1)}), bf16[128,16,64,128]{3,2,1,0:T(8,128)(2,1)}) %all-gather.3.cloned.1.call-update) | async-done | bytes 33554448 | tf_op jit(solution)/shard_map/all_gather | solution.py:19
  511.3 16.4 %reduce_sum.12 = bf16[32,16,64,128]{3,2,1,0:T(8,128)(2,1)} reduce(bf16[4,32,16,64,128]{4,3,2,1,0:T(8,128)(2,1)} %bitcast.211, bf16[]{:T(256)} %constant.55.clone.1), dimensions={0}, to_apply=%region_0.1 | reduce | flops 12582912 | bytes 41943040 | tf_op jit(solution)/shard_map/reduce_sum | solution.py:20
  527.7 11.7 %convert_element_type.97 = f32[32,16,64,128]{3,2,1,0:T(8,128)} convert(bf16[32,16,64,128]{3,2,1,0:T(8,128)(2,1)} %reduce_sum.12) | non-fusion elementwise | flops 4194304 | bytes 25165824 | tf_op jit(solution)/shard_map/convert_element_type | solution.py:133
  (60 shorter events, 67.8 us)
Async XLA Ops:
  34.6 42.0 %copy-start = (f32[16,64,64,32]{2,1,0,3:T(8,128)S(1)}, f32[16,64,64,32]{2,1,0,3:T(8,128)}, u32[]{:S(2)}) copy-start(f32[16,64,64,32]{2,1,0,3:T(8,128)} %reshape.397) | copy-start | bytes 25165828
  122.4 122.1 %all-to-all-start = ((bf16[8,2,32768]{2,1,0:T(2,128)(2,1)}), bf16[8,2,32768]{2,1,0:T(2,128)(2,1)S(1)}, u32[]{:S(2)}, u32[]{:S(2)}) async-start(bf16[8,2,32768]{2,1,0:T(2,128)(2,1)} %reshape.425), calls=%async_computation | async-start | bytes 2097152 | tf_op jit(solution)/shard_map/all_to_all | solution.py:125
  156.9 41.9 %copy-start.1 = (f32[16,64,64,32]{2,1,0,3:T(8,128)S(1)}, f32[16,64,64,32]{2,1,0,3:T(8,128)}, u32[]{:S(2)}) copy-start(f32[16,64,64,32]{2,1,0,3:T(8,128)} %reshape.406) | copy-start | bytes 25165828
  244.5 31.5 %all-to-all-start.2 = ((bf16[8,2,32768]{2,1,0:T(2,128)(2,1)}), bf16[8,2,32768]{2,1,0:T(2,128)(2,1)}, u32[]{:S(2)}, u32[]{:S(2)}) async-start(bf16[8,2,32768]{2,1,0:T(2,128)(2,1)} %reshape.429), calls=%async_computation.2 | async-start | bytes 2097152 | tf_op jit(solution)/shard_map/all_to_all | solution.py:124
  250.5 260.7 %all-gather.3.cloned.1.call-start = ((), (), s32[]{:S(2)}) async-start(), calls=%async_computation.3 | async-start | bytes 41943040 | tf_op jit(solution)/shard_map/all_gather | solution.py:19
  337.6 29.8 %all-to-all-start.1 = ((bf16[8,2,32768]{2,1,0:T(2,128)(2,1)}), bf16[8,2,32768]{2,1,0:T(2,128)(2,1)S(1)}, u32[]{:S(2)}, u32[]{:S(2)}) async-start(bf16[8,2,32768]{2,1,0:T(2,128)(2,1)} %reshape.427), calls=%async_computation.1 | async-start | bytes 2097152 | tf_op jit(solution)/shard_map/all_to_all | solution.py:143
Sparse Core Ops, SparseCore 0:
  310.9 200.2 all-gather.2
